TPU v7x, 512 devices: a whole 4x4x16 slice. The times are simulated.
512 devices in a mesh: gx: 8 (over x, core), gy: 8 (over z_lo), gz: 8 (over z_hi, y).
Axes of the slice: x: 4, y: 4, z: 16 (z_hi: 2, z_lo: 8; z = z_hi * 8 + z_lo), core: 2. Of those that a mesh axis runs over, the one named last changes fastest.
Arguments:
- volume: bfloat16 [4, 32, 64, 1024], P(None, 'gx', 'gy', 'gz'), may hold values from -6 to 6
- act_one: bfloat16 [16, 32, 64, 1024], P(None, 'gx', 'gy', 'gz'), may hold values from -6 to 6
- act_two: bfloat16 [16, 32, 64, 1024], P(None, 'gx', 'gy', 'gz'), may hold values from -6 to 6
- weight_one: bfloat16 [16, 4, 3, 3, 3], replicated, may hold values from -0.625 to 0.625
- weight_two: bfloat16 [16, 16, 3, 3, 3], replicated, may hold values from -0.3125 to 0.3125
- cotangent: bfloat16 [16, 32, 64, 1024], P(None, 'gx', 'gy', 'gz'), may hold values from -18 to 18
Outputs:
- grad_weight_one: float32 [16, 4, 3, 3, 3], replicated
- grad_bias_one: float32 [16], replicated
- grad_weight_two: float32 [16, 16, 3, 3, 3], replicated
- grad_bias_two: float32 [16], replicated
- grad_volume: float32 [4, 32, 64, 1024], P(None, 'gx', 'gy', 'gz')
All inputs are finite; a program needn't handle non-finite values.
Results may differ from a plain program's by a relative error of at most 0.0055.
Values may be sent and summed in bfloat16 or wider, within the bound.
A program may use at most 64 MiB of HBM per device.

v0:
```python
import math

import jax
import jax.numpy as jnp
from jax import lax
from jax.sharding import PartitionSpec as P

CHAN_IN = 4
CHAN = 16


def with_halo(cells, sides, width):
    for axis, dim in sides:
        count = lax.axis_size(axis)
        head = lax.slice_in_dim(cells, 0, width, axis=dim)
        tail = lax.slice_in_dim(cells, cells.shape[dim] - width, cells.shape[dim], axis=dim)
        cells = jnp.concatenate(
            [
                lax.ppermute(tail, axis, [(i, (i + 1) % count) for i in range(count)]),
                cells,
                lax.ppermute(head, axis, [((i + 1) % count, i) for i in range(count)]),
            ],
            axis=dim,
        )
    return cells


def packed_total(arrays, axis):
    ends = [0]
    for a in arrays:
        ends.append(ends[-1] + a.size)
    subtotal = lax.psum(jnp.concatenate([a.ravel() for a in arrays]), axis)
    return tuple((subtotal[b:e].reshape(a.shape) for a, b, e in zip(arrays, ends, ends[1:])))


def slope_of(saved):
    return jnp.where(saved > 0, 1.0, 0.3).astype(jnp.float32)


def tap_list():
    return [(tap_x, tap_y, tap_z) for tap_x in range(3) for tap_y in range(3) for tap_z in range(3)]


def window(padded, start_x, start_y, start_z, extent):
    depth = padded.shape[0]
    piece = lax.slice(
        padded,
        (0, start_x, start_y, start_z),
        (depth, start_x + extent[0], start_y + extent[1], start_z + extent[2]),
    )
    return piece.reshape(depth, -1)


def weight_from_deltas(flat_source, padded_delta, extent):
    columns = []
    for tap_x, tap_y, tap_z in tap_list():
        shifted = window(padded_delta, 2 - tap_x, 2 - tap_y, 2 - tap_z, extent)
        columns.append(
            jnp.einsum("oc,ic->oi", shifted, flat_source, preferred_element_type=jnp.float32)
        )
    return jnp.stack(columns, -1).reshape(padded_delta.shape[0], flat_source.shape[0], 3, 3, 3)


def back_through(weights, padded_delta, extent):
    total = jnp.zeros((weights.shape[1], extent[0] * extent[1] * extent[2]), jnp.float32)
    for tap_x, tap_y, tap_z in tap_list():
        shifted = window(padded_delta, 2 - tap_x, 2 - tap_y, 2 - tap_z, extent)
        total = total + jnp.dot(
            weights[:, :, tap_x, tap_y, tap_z].T, shifted, preferred_element_type=jnp.float32
        )
    return total.reshape((weights.shape[1],) + tuple(extent))


def local(volume, act_one, act_two, weight_one, weight_two, cotangent):
    extent = tuple(volume.shape[1:])
    total_cells = (
        extent[0]
        * extent[1]
        * extent[2]
        * lax.axis_size("gx")
        * lax.axis_size("gy")
        * lax.axis_size("gz")
    )
    norm = 1.0 / math.sqrt(total_cells)
    delta_two = (cotangent.astype(jnp.float32) * slope_of(act_two)).astype(jnp.bfloat16)
    flat_two = delta_two.reshape(CHAN, -1)
    bias_two = jnp.sum(flat_two.astype(jnp.float32), axis=1)
    rims_two = with_halo(delta_two, (("gx", 1), ("gy", 2), ("gz", 3)), 1)
    grad_two = weight_from_deltas(act_one.reshape(CHAN, -1), rims_two, extent)
    back = back_through(weight_two, rims_two, extent)
    delta_one = (back * slope_of(act_one)).astype(jnp.bfloat16)
    flat_one = delta_one.reshape(CHAN, -1)
    rims_one = with_halo(delta_one, (("gx", 1), ("gy", 2), ("gz", 3)), 1)
    grad_one = weight_from_deltas(volume.reshape(CHAN_IN, -1), rims_one, extent)
    bias_one = jnp.sum(flat_one.astype(jnp.float32), axis=1)
    grad_volume = back_through(weight_one, rims_one, extent)
    grad_one, bias_one, grad_two, bias_two = packed_total(
        (grad_one, bias_one, grad_two, bias_two), ("gx", "gy", "gz")
    )
    return (grad_one * norm, bias_one * norm, grad_two * norm, bias_two * norm, grad_volume)


def solution(mesh):
    placed = (
        P(None, "gx", "gy", "gz"),
        P(None, "gx", "gy", "gz"),
        P(None, "gx", "gy", "gz"),
        P(),
        P(),
        P(None, "gx", "gy", "gz"),
    )
    return jax.shard_map(
        local,
        mesh=mesh,
        in_specs=placed,
        out_specs=(P(), P(), P(), P(), P(None, "gx", "gy", "gz")),
        check_vma=False,
    )
```

profile of v0, /device:TPU:1, one launch (start us, length us, event | category | flops | bytes accessed | tf_op | source)
XLA Modules:
  0.0 254.7 jit_solution(2380595459567346899)
XLA Ops:
  0.6 1.2 convert_reduce_fusion
  1.8 2.6 %collective-permute-start = (bf16[16,1,8,128]{3,0,2,1:T(8,128)(2,1)S(1)}, bf16[16,1,8,128]{3,0,2,1:T(8,128)(2,1)S(1)}, u32[]{:S(2)}, u32[]{:S(2)}) collective-permute-start(bf16[16,1,8,128]{3,0,2,1:T(8,128)(2,1)S(1)} %get-tuple-element.84), channel_id=1, source_target_pairs={{0,64},{64,128},{128,192},{192,256},{256,320},{320,384},{384,448},... | collective-permute-start | bytes 98312 | tf_op jit(solution)/shard_map/ppermute | solution.py:19
  4.4 4.3 %collective-permute-start.1 = (bf16[16,1,8,128]{3,0,2,1:T(8,128)(2,1)S(1)}, bf16[16,1,8,128]{3,0,2,1:T(8,128)(2,1)S(1)}, u32[]{:S(2)}, u32[]{:S(2)}) collective-permute-start(bf16[16,1,8,128]{3,0,2,1:T(8,128)(2,1)S(1)} %get-tuple-element.85), channel_id=1, source_target_pairs={{64,0},{128,64},{192,128},{256,192},{320,256},{384,320},{448,384},... | collective-permute-start | bytes 98312 | tf_op jit(solution)/shard_map/ppermute | solution.py:21
  8.8 0.6 collective-permute-done
  9.6 1.9 collective-permute-start.2
  11.5 11.1 %collective-permute-start.3 = (bf16[16,6,1,128]{3,0,2,1:T(8,128)(2,1)S(1)}, bf16[16,6,1,128]{3,0,2,1:T(8,128)(2,1)S(1)}, u32[]{:S(2)}, u32[]{:S(2)}) collective-permute-start(bf16[16,6,1,128]{3,0,2,1:T(8,128)(2,1)S(1)} %get-tuple-element.77), channel_id=1, source_target_pairs={{8,0},{16,8},{24,16},{32,24},{40,32},{48,40},{56,48},{0,56},{9,1},... | collective-permute-start | bytes 73736 | tf_op jit(solution)/shard_map/ppermute | solution.py:21
  22.7 0.8 collective-permute-done.3
  23.7 3.2 %collective-permute-start.5 = (bf16[16,6,10,1]{3,0,2,1:T(8,128)(2,1)S(1)}, bf16[16,6,10,1]{3,0,2,1:T(8,128)(2,1)S(1)}, u32[]{:S(2)}, u32[]{:S(2)}) collective-permute-start(bf16[16,6,10,1]{3,0,2,1:T(8,128)(2,1)S(1)} %get-tuple-element.56), channel_id=1, source_target_pairs={{0,1},{1,2},{2,3},{3,4},{4,5},{5,6},{6,7},{7,0},{8,9},{9,10},{10,1... | collective-permute-start | bytes 5768 | tf_op jit(solution)/shard_map/ppermute | solution.py:19
  26.9 13.7 %collective-permute-start.4 = (bf16[16,6,10,1]{3,0,2,1:T(8,128)(2,1)S(1)}, bf16[16,6,10,1]{3,0,2,1:T(8,128)(2,1)S(1)}, u32[]{:S(2)}, u32[]{:S(2)}) collective-permute-start(bf16[16,6,10,1]{3,0,2,1:T(8,128)(2,1)S(1)} %get-tuple-element.57), channel_id=1, source_target_pairs={{1,0},{2,1},{3,2},{4,3},{5,4},{6,5},{7,6},{0,7},{9,8},{10,9},{11,1... | collective-permute-start | bytes 5768 | tf_op jit(solution)/shard_map/ppermute | solution.py:21
  41.1 18.6 %collective-permute-done.5 = bf16[16,6,10,1]{3,0,2,1:T(8,128)(2,1)S(1)} collective-permute-done((bf16[16,6,10,1]{3,0,2,1:T(8,128)(2,1)S(1)}, bf16[16,6,10,1]{3,0,2,1:T(8,128)(2,1)S(1)}, u32[]{:S(2)}, u32[]{:S(2)}) %collective-permute-start.5) | collective-permute-done | bytes 1952 | tf_op jit(solution)/shard_map/ppermute | solution.py:19
  59.8 1.2 collective-permute-done.4
  60.9 0.3 maximum_maximum_fusion
  61.5 0.6 fusion.406
  62.4 0.2 fusion.48
  63.1 0.2 fusion.46
  63.7 0.2 fusion.44
  64.3 0.2 fusion.42
  65.0 0.2 fusion.39
  65.6 0.2 fusion.37
  66.2 0.2 fusion.35
  66.8 0.2 fusion.33
  67.9 0.4 copy-done.8
  74.6 0.3 convert_reduce_fusion.1
  74.9 2.8 %collective-permute-start.6 = (bf16[16,1,8,128]{3,0,2,1:T(8,128)(2,1)S(1)}, bf16[16,1,8,128]{3,0,2,1:T(8,128)(2,1)S(1)}, u32[]{:S(2)}, u32[]{:S(2)}) collective-permute-start(bf16[16,1,8,128]{3,0,2,1:T(8,128)(2,1)S(1)} %get-tuple-element.80), channel_id=1, source_target_pairs={{0,64},{64,128},{128,192},{192,256},{256,320},{320,384},{384,448},... | collective-permute-start | bytes 98312 | tf_op jit(solution)/shard_map/ppermute | solution.py:19
  78.7 2.3 collective-permute-done.7
  81.0 1.9 collective-permute-start.8
  83.0 10.0 %collective-permute-start.9 = (bf16[16,6,1,128]{3,0,2,1:T(8,128)(2,1)S(1)}, bf16[16,6,1,128]{3,0,2,1:T(8,128)(2,1)S(1)}, u32[]{:S(2)}, u32[]{:S(2)}) collective-permute-start(bf16[16,6,1,128]{3,0,2,1:T(8,128)(2,1)S(1)} %get-tuple-element.73), channel_id=1, source_target_pairs={{8,0},{16,8},{24,16},{32,24},{40,32},{48,40},{56,48},{0,56},{9,1},... | collective-permute-start | bytes 73736 | tf_op jit(solution)/shard_map/ppermute | solution.py:21
  93.0 0.7 copy.160
  94.0 1.9 collective-permute-start.11
  96.0 20.3 %collective-permute-start.10 = (bf16[16,6,10,1]{3,0,2,1:T(8,128)(2,1)S(1)}, bf16[16,6,10,1]{3,0,2,1:T(8,128)(2,1)S(1)}, u32[]{:S(2)}, u32[]{:S(2)}) collective-permute-start(bf16[16,6,10,1]{3,0,2,1:T(8,128)(2,1)S(1)} %get-tuple-element.53), channel_id=1, source_target_pairs={{1,0},{2,1},{3,2},{4,3},{5,4},{6,5},{7,6},{0,7},{9,8},{10,9},{11,1... | collective-permute-start | bytes 5768 | tf_op jit(solution)/shard_map/ppermute | solution.py:21
  116.5 0.7 copy.172
  117.1 0.7 copy.163
  117.9 0.7 copy.166
  118.6 0.7 copy.157
  119.4 0.3 maximum_maximum_fusion.1
  120.2 0.2 fusion.75
  120.8 0.2 fusion.73
  121.4 0.2 fusion.71
  121.9 0.2 fusion.69
  125.1 117.7 %psum.7 = f32[8672]{0:T(1024)S(1)} all-reduce(f32[8672]{0:T(1024)S(1)} %concatenate.109), channel_id=1, replica_groups=mesh['gx'=8,'gy'=8,'gz'=8] {'gx','gy','gz'}, use_global_device_ids=true, to_apply=%region_2.3 | all-reduce | flops 8672 | bytes 69376 | tf_op jit(solution)/shard_map/psum | solution.py:32
  242.9 0.6 slice_multiply_fusion.2
  243.5 0.7 slice_multiply_fusion
  244.3 0.4 fusion.405
  244.7 0.3 mul.34
  245.0 0.9 copy.183
  251.5 0.6 copy.630
  252.1 0.8 mul.38
  253.0 1.8 copy.184
  (195 shorter events, 22.4 us)
Async XLA Ops:
  0.6 119.1 %copy-start = (bf16[4,4,8,128]{3,2,1,0:T(8,128)(2,1)S(1)}, bf16[4,4,8,128]{3,2,1,0:T(8,128)(2,1)}, u32[]{:S(2)}) copy-start(bf16[4,4,8,128]{3,2,1,0:T(8,128)(2,1)} %param.6) | copy-start | bytes 98308
  1.8 7.6 %collective-permute-start = (bf16[16,1,8,128]{3,0,2,1:T(8,128)(2,1)S(1)}, bf16[16,1,8,128]{3,0,2,1:T(8,128)(2,1)S(1)}, u32[]{:S(2)}, u32[]{:S(2)}) collective-permute-start(bf16[16,1,8,128]{3,0,2,1:T(8,128)(2,1)S(1)} %get-tuple-element.84), channel_id=1, source_target_pairs={{0,64},{64,128},{128,192},{192,256},{256,320},{320,384},{384,448},... | collective-permute-start | bytes 98312 | tf_op jit(solution)/shard_map/ppermute | solution.py:19
  4.4 5.1 %collective-permute-start.1 = (bf16[16,1,8,128]{3,0,2,1:T(8,128)(2,1)S(1)}, bf16[16,1,8,128]{3,0,2,1:T(8,128)(2,1)S(1)}, u32[]{:S(2)}, u32[]{:S(2)}) collective-permute-start(bf16[16,1,8,128]{3,0,2,1:T(8,128)(2,1)S(1)} %get-tuple-element.85), channel_id=1, source_target_pairs={{64,0},{128,64},{192,128},{256,192},{320,256},{384,320},{448,384},... | collective-permute-start | bytes 98312 | tf_op jit(solution)/shard_map/ppermute | solution.py:21
  9.6 13.1 %collective-permute-start.2 = (bf16[16,6,1,128]{3,0,2,1:T(8,128)(2,1)S(1)}, bf16[16,6,1,128]{3,0,2,1:T(8,128)(2,1)S(1)}, u32[]{:S(2)}, u32[]{:S(2)}) collective-permute-start(bf16[16,6,1,128]{3,0,2,1:T(8,128)(2,1)S(1)} %get-tuple-element.76), channel_id=1, source_target_pairs={{0,8},{8,16},{16,24},{24,32},{32,40},{40,48},{48,56},{56,0},{1,9},... | collective-permute-start | bytes 73736 | tf_op jit(solution)/shard_map/ppermute | solution.py:19
  11.5 12.0 %collective-permute-start.3 = (bf16[16,6,1,128]{3,0,2,1:T(8,128)(2,1)S(1)}, bf16[16,6,1,128]{3,0,2,1:T(8,128)(2,1)S(1)}, u32[]{:S(2)}, u32[]{:S(2)}) collective-permute-start(bf16[16,6,1,128]{3,0,2,1:T(8,128)(2,1)S(1)} %get-tuple-element.77), channel_id=1, source_target_pairs={{8,0},{16,8},{24,16},{32,24},{40,32},{48,40},{56,48},{0,56},{9,1},... | collective-permute-start | bytes 73736 | tf_op jit(solution)/shard_map/ppermute | solution.py:21
  23.7 36.0 %collective-permute-start.5 = (bf16[16,6,10,1]{3,0,2,1:T(8,128)(2,1)S(1)}, bf16[16,6,10,1]{3,0,2,1:T(8,128)(2,1)S(1)}, u32[]{:S(2)}, u32[]{:S(2)}) collective-permute-start(bf16[16,6,10,1]{3,0,2,1:T(8,128)(2,1)S(1)} %get-tuple-element.56), channel_id=1, source_target_pairs={{0,1},{1,2},{2,3},{3,4},{4,5},{5,6},{6,7},{7,0},{8,9},{9,10},{10,1... | collective-permute-start | bytes 5768 | tf_op jit(solution)/shard_map/ppermute | solution.py:19
  26.9 34.0 %collective-permute-start.4 = (bf16[16,6,10,1]{3,0,2,1:T(8,128)(2,1)S(1)}, bf16[16,6,10,1]{3,0,2,1:T(8,128)(2,1)S(1)}, u32[]{:S(2)}, u32[]{:S(2)}) collective-permute-start(bf16[16,6,10,1]{3,0,2,1:T(8,128)(2,1)S(1)} %get-tuple-element.57), channel_id=1, source_target_pairs={{1,0},{2,1},{3,2},{4,3},{5,4},{6,5},{7,6},{0,7},{9,8},{10,9},{11,1... | collective-permute-start | bytes 5768 | tf_op jit(solution)/shard_map/ppermute | solution.py:21
  40.9 20.4 %copy-start.6 = (bf16[16,4,8,128]{3,2,1,0:T(8,128)(2,1)S(1)}, bf16[16,4,8,128]{3,2,1,0:T(8,128)(2,1)}, u32[]{:S(2)}) copy-start(bf16[16,4,8,128]{3,2,1,0:T(8,128)(2,1)} %param.7) | copy-start | bytes 393220
  67.3 0.9 copy-start.8
  74.9 3.8 %collective-permute-start.6 = (bf16[16,1,8,128]{3,0,2,1:T(8,128)(2,1)S(1)}, bf16[16,1,8,128]{3,0,2,1:T(8,128)(2,1)S(1)}, u32[]{:S(2)}, u32[]{:S(2)}) collective-permute-start(bf16[16,1,8,128]{3,0,2,1:T(8,128)(2,1)S(1)} %get-tuple-element.80), channel_id=1, source_target_pairs={{0,64},{64,128},{128,192},{192,256},{256,320},{320,384},{384,448},... | collective-permute-start | bytes 98312 | tf_op jit(solution)/shard_map/ppermute | solution.py:19
  77.7 3.3 %collective-permute-start.7 = (bf16[16,1,8,128]{3,0,2,1:T(8,128)(2,1)S(1)}, bf16[16,1,8,128]{3,0,2,1:T(8,128)(2,1)S(1)}, u32[]{:S(2)}, u32[]{:S(2)}) collective-permute-start(bf16[16,1,8,128]{3,0,2,1:T(8,128)(2,1)S(1)} %get-tuple-element.81), channel_id=1, source_target_pairs={{64,0},{128,64},{192,128},{256,192},{320,256},{384,320},{448,384},... | collective-permute-start | bytes 98312 | tf_op jit(solution)/shard_map/ppermute | solution.py:21
  81.0 12.7 %collective-permute-start.8 = (bf16[16,6,1,128]{3,0,2,1:T(8,128)(2,1)S(1)}, bf16[16,6,1,128]{3,0,2,1:T(8,128)(2,1)S(1)}, u32[]{:S(2)}, u32[]{:S(2)}) collective-permute-start(bf16[16,6,1,128]{3,0,2,1:T(8,128)(2,1)S(1)} %get-tuple-element.72), channel_id=1, source_target_pairs={{0,8},{8,16},{16,24},{24,32},{32,40},{40,48},{48,56},{56,0},{1,9},... | collective-permute-start | bytes 73736 | tf_op jit(solution)/shard_map/ppermute | solution.py:19
  83.0 10.9 %collective-permute-start.9 = (bf16[16,6,1,128]{3,0,2,1:T(8,128)(2,1)S(1)}, bf16[16,6,1,128]{3,0,2,1:T(8,128)(2,1)S(1)}, u32[]{:S(2)}, u32[]{:S(2)}) collective-permute-start(bf16[16,6,1,128]{3,0,2,1:T(8,128)(2,1)S(1)} %get-tuple-element.73), channel_id=1, source_target_pairs={{8,0},{16,8},{24,16},{32,24},{40,32},{48,40},{56,48},{0,56},{9,1},... | collective-permute-start | bytes 73736 | tf_op jit(solution)/shard_map/ppermute | solution.py:21
  94.0 25.2 %collective-permute-start.11 = (bf16[16,6,10,1]{3,0,2,1:T(8,128)(2,1)S(1)}, bf16[16,6,10,1]{3,0,2,1:T(8,128)(2,1)S(1)}, u32[]{:S(2)}, u32[]{:S(2)}) collective-permute-start(bf16[16,6,10,1]{3,0,2,1:T(8,128)(2,1)S(1)} %get-tuple-element.52), channel_id=1, source_target_pairs={{0,1},{1,2},{2,3},{3,4},{4,5},{5,6},{6,7},{7,0},{8,9},{9,10},{10,1... | collective-permute-start | bytes 5768 | tf_op jit(solution)/shard_map/ppermute | solution.py:19
  96.0 23.4 %collective-permute-start.10 = (bf16[16,6,10,1]{3,0,2,1:T(8,128)(2,1)S(1)}, bf16[16,6,10,1]{3,0,2,1:T(8,128)(2,1)S(1)}, u32[]{:S(2)}, u32[]{:S(2)}) collective-permute-start(bf16[16,6,10,1]{3,0,2,1:T(8,128)(2,1)S(1)} %get-tuple-element.53), channel_id=1, source_target_pairs={{1,0},{2,1},{3,2},{4,3},{5,4},{6,5},{7,6},{0,7},{9,8},{10,9},{11,1... | collective-permute-start | bytes 5768 | tf_op jit(solution)/shard_map/ppermute | solution.py:21
  246.2 0.7 copy-start.9
  246.3 0.9 copy-start.5
  246.4 1.3 copy-start.1
  246.6 1.6 copy-start.4
  246.7 2.0 copy-start.3
  247.7 2.0 copy-start.2
  249.7 2.5 copy-start.7
where the time goes:
time: 255 us
  blocking collectives  118 us (46%)
  starting transfers between devices  73.6 us (29%)
  waiting for transfers between devices  24.3 us (10%)
  matrix products  20.9 us (8%)
  local copies, waits for them, and re-layouts  12.8 us (5%)
  other arithmetic  3.72 us (1%)
    psum x1, blocking collectives, packed_total(): subtotal = lax.psum(jnp.concatenate([a.ravel() for a in arrays]), axis)  118 us
    ppermute x6, starting transfers between devices, with_halo(): lax.ppermute(head, axis, [((i + 1) % count, i) for i in range(count)])  59.3 us
    ppermute x6, waiting for transfers between devices, with_halo(): lax.ppermute(tail, axis, [(i, (i + 1) % count) for i in range(count)])  19.5 us
    ppermute x6, starting transfers between devices, with_halo(): lax.ppermute(tail, axis, [(i, (i + 1) % count) for i in range(count)])  14.3 us
    dot_general x54, matrix products, weight_from_deltas(): jnp.einsum('oc,ic->oi', shifted, flat_source, preferred_element_type=jnp....  10.6 us
    dot_general x54, matrix products, back_through(): jnp.dot(weights[:, :, tap_x, tap_y, tap_z].T, shifted, preferred_element_...  10.3 us
    slice x58, local copies, waits for them, and re-layouts, window(): lax.slice(padded, (0, start_x, start_y, start_z), (depth, start_x + exten...  6.49 us
  transfers between devices with their start and end apart: 12, of which 9 were waited for; matrix products, arithmetic and copies ran while one was open for 2% of the time, Pallas kernels for 0%

commit v1 on v0

v1 whole, which is shorter than its diff:
```python
import functools
import math

import jax
import jax.numpy as jnp
import numpy as np
from jax import lax
from jax.experimental import pallas as pl
from jax.experimental.pallas import tpu as pltpu
from jax.sharding import PartitionSpec as P

CHAN_IN = 4
CHAN = 16
NX, NY, NZ = 4, 8, 128
F32, BF16 = jnp.float32, jnp.bfloat16
MESH = pl.DeviceIdType.MESH
ROWS = 3
SIDES = ((-1, 0), (1, 0), (0, -1), (0, 1), (-1, -1), (-1, 1), (1, -1), (1, 1))


def constants():
    r = np.arange(128)
    perm = np.zeros((128, 128), np.float32)
    perm[r, (r % 16) * 8 + r // 16] = 1
    eye = np.eye(128, dtype=np.float32)
    ends = np.zeros((16, 128), np.float32)
    ends[0, 0] = ends[1, 127] = 1
    tiles = np.zeros((32, 128), np.float32)
    for h in range(2):
        for x in range(4):
            for j in range(4):
                tiles[h * 16 + x * 4 + j, j * 32 + x * 8 + 7 * h] = 1
    rim_cols = np.zeros((48, 128), np.float32)
    rim_rows = np.zeros((48, 128), np.float32)
    for p in range(6):
        x = (p - 1) % 4
        for h in range(2):
            for j in range(4):
                rim_cols[p * 8 + h * 4 + j, j * 32 + x * 8 + 7 * (1 - h)] = 1
                tile = h if 1 <= p <= 4 else 2 + (0 if p == 0 else 2) + h
                rim_rows[p * 8 + h * 4 + j, tile * 16 + x * 4 + j] = 1
    spread = np.zeros((128, 128), np.float32)
    spread[r, r % 16] = 1
    narrow = np.concatenate([perm, eye, ends, tiles, rim_cols, rim_rows, spread])
    lane = np.arange(512)
    inside = lane < 480
    tap, end, chan = lane // 160, (lane % 160) // 16, lane % 16
    place = np.zeros((48, 512), np.float32)
    for c in range(3):
        for o in range(16):
            place[c * 16 + o] = inside & (tap == c) & (chan == o)
    y_two = (np.arange(128) // 16)[:, None]
    y_one = (np.arange(32) % 8)[:, None]
    band_two = np.where(inside[None], y_two + 2 - end[None], -9)
    band_one = np.where(inside[None], y_one + 2 - end[None], -9)
    wide = np.concatenate([place, band_two, band_one])
    rr = np.arange(128) % 40
    ok = np.arange(128) < 120
    row_y = np.where(rr < 32, 1 + rr % 8, np.where(rr < 36, 0, 9))
    row_j = np.where(rr < 32, rr // 8, rr % 4)
    row_c = np.arange(128) // 40
    y_of = np.broadcast_to(np.where(ok, row_y, -9)[None], (16, 128))
    fold = np.zeros((9, 128, 128), np.float32)
    for ab in range(9):
        for q in range(120):
            fold[ab, q, (ab * 3 + row_c[q]) * 4 + row_j[q]] = 1
    narrow = np.concatenate([narrow, y_of, fold.reshape(-1, 128)])
    return jnp.asarray(narrow, BF16), jnp.asarray(wide, BF16)


AT = {}
_at = 0
for _name, _n in (("perm", 128), ("eye", 128), ("ends", 16), ("tiles", 32), ("rim_cols", 48), ("rim_rows", 48), ("spread", 128), ("y_of", 16), ("fold", 1152)):
    AT[_name] = (_at, _n)
    _at += _n
NARROW = _at


def nt(a, b):
    return lax.dot_general(a, b, (((1,), (1,)), ((), ())), preferred_element_type=F32)


def nn(a, b):
    return jnp.dot(a, b, preferred_element_type=F32)


def way(dx, dy):
    return (dx + 1) * 3 + dy + 1


def corner(dx, dy):
    return (dx + 1) + (dy + 1) // 2


def kernel(
    sizes, norm,
    vol_h, act1_h, act2_h, w1_h, w2_h, cot_h, narrow_h, wide_h,
    gw1, gb1, gw2, gb2, gvol,
    vol_v, act1_v, act2_v, w1_v, w2_v, cot_v, narrow_v, wide_v,
    xs, xr, ys, yr, xyr, zs, zr,
    xs2, xr2, ys2, yr2, xyr2, zs2, zr2,
    inner, acts, planes, volp, m_two, m_one, share, got1, got2, mid1, mid2, summed,
    load_sem, own_sem, send_sem, recv_sem, red_send, red_recv,
):
    n_gx, n_gy, n_gz = sizes
    n_y = 4
    n_hi = n_gz // n_y
    n_group = n_gx * n_y
    n_line = n_gy * n_hi
    gx, gy, gz = lax.axis_index("gx"), lax.axis_index("gy"), lax.axis_index("gz")
    y_pos, hi_pos = lax.rem(gz, n_y), lax.div(gz, n_y)
    group_at = gx * n_y + y_pos
    line_at = hi_pos * n_gy + gy

    def near(dx, dy, dz):
        return (
            lax.rem(gx + (n_gx + dx), n_gx),
            lax.rem(gy + (n_gy + dy), n_gy),
            lax.rem(gz + (n_gz + dz), n_gz),
        )

    def in_group(k):
        t = lax.rem(group_at + k, n_group)
        return t, (lax.div(t, n_y), gy, hi_pos * n_y + lax.rem(t, n_y))

    def in_line(k):
        t = lax.rem(line_at + k, n_line)
        return t, (gx, lax.rem(t, n_gy), lax.div(t, n_gy) * n_y + y_pos)

    barrier = pltpu.get_barrier_semaphore()
    for dz in (-1, 1, 0):
        for dx in (-1, 0, 1):
            for dy in (-1, 0, 1):
                if (dx, dy, dz) != (0, 0, 0):
                    pl.semaphore_signal(barrier, inc=1, device_id=near(dx, dy, dz), device_id_type=MESH)

    def greet_line(k, _):
        pl.semaphore_signal(barrier, inc=1, device_id=in_line(k)[1], device_id_type=MESH)
        return 0

    def greet_group(k, _):
        pl.semaphore_signal(barrier, inc=1, device_id=in_group(k)[1], device_id_type=MESH)
        return 0

    lax.fori_loop(1, n_line, greet_line, 0)
    lax.fori_loop(1, n_group, greet_group, 0)

    loads = [
        pltpu.make_async_copy(src, dst, load_sem.at[i])
        for i, (src, dst) in enumerate(
            ((cot_h, cot_v), (act2_h, act2_v), (narrow_h, narrow_v), (vol_h, vol_v), (act1_h, act1_v), (wide_h, wide_v), (w2_h, w2_v), (w1_h, w1_v))
        )
    ]
    for copy in loads:
        copy.start()

    def const(name):
        at, n = AT[name]
        return narrow_v[at : at + n, :]

    for i in range(4):
        loads[i].wait()
    perm, eye, ends = const("perm"), const("eye"), const("ends")

    def rows_of(ref, x):
        return ref[:, x].astype(F32).reshape(128, 128)

    def edge_rows(inner_at):
        return jnp.concatenate(
            [inner_at(x)[0:16] for x in range(4)] + [inner_at(x)[112:128] for x in range(4)], axis=0
        )

    row8 = lax.broadcasted_iota(jnp.int32, (8, 128), 0)

    def stack8(rows):
        out = jnp.zeros((8, 128), F32)
        for i, row in enumerate(rows):
            out = jnp.where(row8 == i, jnp.broadcast_to(row, (8, 128)), out)
        return out

    deltas = []
    for x in range(4):
        v = rows_of(cot_v, x)
        deltas.append(jnp.where(rows_of(act2_v, x) > 0, v, v * 0.3).astype(BF16))
    turned = nn(perm, jnp.concatenate(deltas, axis=1))
    bias_two = turned[:, 0:128] + turned[:, 128:256] + turned[:, 256:384] + turned[:, 384:512]
    turned = turned.astype(BF16)
    for x in range(4):
        inner[x] = turned[:, x * 128 : (x + 1) * 128]
    volflat = vol_v[...].astype(F32).reshape(128, 128).astype(BF16)
    vol_tiles = nn(const("tiles"), volflat).astype(BF16)

    def vol_rows(x):
        return vol_v[:, x].astype(F32).reshape(32, 128)

    xs[0, 0:128] = inner[0]
    xs[1, 0:128] = inner[3]
    xs[0, 128:160] = vol_rows(0).astype(BF16)
    xs[1, 128:160] = vol_rows(3).astype(BF16)
    for h in range(2):
        for at, x in ((0, 0), (2, 3), (3, 1), (4, 2)):
            ys[h, at * 16 : at * 16 + 16] = inner[x][112 * h : 112 * h + 16]
        ys[h, 16:32] = vol_tiles[16 * h : 16 * h + 16]
    z_face = nt(ends, jnp.concatenate([inner[x] for x in range(4)], axis=0))
    z_edge = nt(ends, edge_rows(lambda x: inner[x]))
    z_vol = nt(ends, volflat)
    for f in range(2):
        face = [z_face[f : f + 1, x * 128 : (x + 1) * 128] for x in range(4)]
        edge, flat = z_edge[f : f + 1], z_vol[f : f + 1]
        zs[f] = stack8([face[1], face[2], face[0], flat, face[3], edge, flat])

    pl.semaphore_wait(barrier, 26 + (n_line - 1) + (n_group - 1))

    def exchange(phase, xs, xr, ys, yr, xyr, zs, zr):
        first = phase == 0
        out = []

        def send(kind, src, dst, where):
            copy = pltpu.make_async_remote_copy(
                src, dst, send_sem.at[phase, kind], recv_sem.at[phase, kind], device_id=where, device_id_type=MESH
            )
            copy.start()
            out.append(copy)

        for dz in (-1, 1):
            f, side = (1 if dz == 1 else 0), (0 if dz == 1 else 1)
            for dx in (-1, 0, 1):
                for dy in (-1, 0, 1):
                    if first:
                        at, n = {-1: (2, 2), 1: (3, 2), 0: (0, 5) if dy == 0 else (5, 2)}[dx]
                    else:
                        at, n = {-1: (2, 1), 1: (3, 1), 0: (0, 4) if dy == 0 else (4, 1)}[dx]
                    send(0, zs.at[f, pl.ds(at, n)], zr.at[side, pl.ds(8 * way(-dx, -dy), n)], near(dx, dy, dz))
        for dx in (-1, 1):
            send(1, xs.at[(dx + 1) // 2], xr.at[(1 - dx) // 2], near(dx, 0, 0))
        for dy in (-1, 1):
            send(2, ys.at[(dy + 1) // 2], yr.at[(1 - dy) // 2], near(0, dy, 0))
        for dx in (-1, 1):
            for dy in (-1, 1):
                if first:
                    at, n = (0 if dx == -1 else 16), 32
                else:
                    at, n = (0 if dx == -1 else 16), 16
                send(3, ys.at[(dy + 1) // 2, pl.ds(at, n)], xyr.at[corner(-dx, -dy)], near(dx, dy, 0))

    def settle(sems, phase, xr, yr, xyr, zr):
        n = 42 if phase == 0 else 24
        for kind, ref in ((0, zr.at[0, pl.ds(0, n)]), (1, xr), (2, yr), (3, xyr)):
            pltpu.make_async_copy(ref, ref, sems.at[phase, kind]).wait()

    lane_of = lax.broadcasted_iota(jnp.int32, (160, 128), 1)

    def build_planes(phase, inner_at, xr, yr, xyr, zr):
        first = phase == 0
        cols = nt(eye, zr[...].reshape(144, 128).astype(BF16))
        tile_at = {0: 0, 3: 2, 1: 3, 2: 4} if first else {0: 0, 3: 1, 1: 2, 2: 3}
        face_at = {0: 2, 3: 4, 1: 0, 2: 1} if first else {0: 2, 3: 3, 1: 0, 2: 1}
        for p in range(6):
            if 1 <= p <= 4:
                x = p - 1
                low = yr[0, tile_at[x] * 16 : tile_at[x] * 16 + 16]
                mid = inner_at(x)
                high = yr[1, tile_at[x] * 16 : tile_at[x] * 16 + 16]
                pick = (
                    (64 + 16 * x, 80 + 16 * x, 8 * way(0, -1)),
                    (0, 128, 8 * way(0, 0) + face_at[x]),
                    (16 * x, 16 * x + 16, 8 * way(0, 1)),
                )
            else:
                dx = -1 if p == 0 else 1
                at = (16 if dx == -1 else 0) if first else 0
                low = xyr[corner(dx, -1), at : at + 16]
                mid = xr[(dx + 1) // 2, 0:128]
                high = xyr[corner(dx, 1), at : at + 16]
                r = (1 if dx == -1 else 0) if first else 0
                pick = (
                    (112, 128, 8 * way(dx, -1) + r),
                    (0, 128, 8 * way(dx, 0) + r),
                    (0, 16, 8 * way(dx, 1) + r),
                )
            plane = jnp.concatenate([low, mid, high], axis=0)
            lanes = slice(p * 128, (p + 1) * 128)
            planes[160:320, lanes] = plane
            plane = plane.astype(F32)
            for tap, side, turn, lane in ((0, 1, 127, 127), (2, 0, 1, 0)):
                col = jnp.concatenate(
                    [cols[a:b, 72 * side + k : 72 * side + k + 1] for a, b, k in pick], axis=0
                )
                shifted = jnp.where(lane_of == lane, jnp.broadcast_to(col, (160, 128)), pltpu.roll(plane, turn, 1))
                planes[tap * 160 : tap * 160 + 160, lanes] = shifted.astype(BF16)
        return cols

    exchange(0, xs, xr, ys, yr, xyr, zs, zr)

    for i in range(4, 8):
        loads[i].wait()
    turned = nn(perm, jnp.concatenate([rows_of(act1_v, x).astype(BF16) for x in range(4)], axis=1))
    acts[...] = turned.astype(BF16)
    planes[480:512, :] = jnp.zeros((32, 768), BF16)
    place = wide_v[0:48, :]
    band_two = wide_v[48:176, :].astype(F32)
    band_one = wide_v[176:208, :].astype(F32)
    spread = const("spread")[:, 0:16]
    for a in range(3):
        total_two = jnp.zeros((128, 512), F32)
        total_one = jnp.zeros((32, 512), F32)
        for b in range(3):
            t = (a * 3 + b) * 3
            group = w2_v[t : t + 3].reshape(48, 16)
            wide = nn(nt(spread, group).astype(BF16), place)
            total_two = jnp.where(band_two == b, wide, total_two)
            four = jnp.zeros((4, 512), F32)
            for c in range(3):
                four = four + nn(w1_v[t + c], place[c * 16 : c * 16 + 16])
            wide = jnp.concatenate([jnp.broadcast_to(four[j : j + 1], (8, 512)) for j in range(4)], axis=0)
            total_one = jnp.where(band_one == b, wide, total_one)
        m_two[a] = total_two.astype(BF16)
        m_one[a] = total_one.astype(BF16)

    settle(recv_sem, 0, xr, yr, xyr, zr)
    cols = build_planes(0, lambda x: inner[x], xr, yr, xyr, zr)

    back = nn(m_two[0], planes[:, 256:768]) + nn(m_two[1], planes[:, 128:640]) + nn(m_two[2], planes[:, 0:512])
    delta = jnp.where(acts[...].astype(F32) > 0, back, back * 0.3).astype(BF16)
    wide_delta = delta.astype(F32)
    bias_one = wide_delta[:, 0:128] + wide_delta[:, 128:256] + wide_delta[:, 256:384] + wide_delta[:, 384:512]

    def delta_at(x):
        return delta[:, x * 128 : (x + 1) * 128]

    xs2[0] = delta_at(0)
    xs2[1] = delta_at(3)
    for h in range(2):
        for at, x in ((0, 0), (1, 3), (2, 1), (3, 2)):
            ys2[h, at * 16 : at * 16 + 16] = delta_at(x)[112 * h : 112 * h + 16]
    z_face = nt(ends, jnp.concatenate([delta_at(x) for x in range(4)], axis=0))
    z_edge = nt(ends, edge_rows(delta_at))
    for f in range(2):
        face = [z_face[f : f + 1, x * 128 : (x + 1) * 128] for x in range(4)]
        zs2[f] = stack8([face[1], face[2], face[0], face[3], z_edge[f : f + 1]])
    exchange(1, xs2, xr2, ys2, yr2, xyr2, zs2, zr2)
    for x in range(4):
        inner[x] = delta_at(x)

    v_tiles = jnp.concatenate(
        [yr[0, 16:32], yr[1, 16:32]]
        + [xyr[corner(dx, dy), at : at + 16] for dx, at in ((-1, 0), (1, 16)) for dy in (-1, 1)],
        axis=0,
    )
    rims = nn(const("rim_rows")[:, 0:96], v_tiles)
    rim_cols = nn(const("rim_cols"), cols.astype(BF16))
    lane40 = lax.broadcasted_iota(jnp.int32, (40, 128), 1)
    half8 = lax.broadcasted_iota(jnp.int32, (8, 1), 0) < 4
    volp[120:128, :] = jnp.zeros((8, 768), F32)
    for p in range(6):
        x = (p - 1) % 4
        dx = -1 if p == 0 else (1 if p == 5 else 0)
        mid = vol_rows(x) if dx == 0 else xr[(dx + 1) // 2, 128:160].astype(F32)
        plane = jnp.concatenate([mid, rims[p * 8 : p * 8 + 8]], axis=0)
        lanes = slice(p * 128, (p + 1) * 128)
        volp[40:80, lanes] = plane
        r = {-1: 0, 1: 1, 0: 1}[dx]
        for tap, side, turn, lane in ((0, 0, 1, 0), (2, 1, 127, 127)):
            k = 72 * side + 8 * way(dx, 0) + (3 if dx == 0 else r)
            col = jnp.concatenate(
                [cols[j * 32 + x * 8 : j * 32 + x * 8 + 8, k : k + 1] for j in range(4)]
                + [
                    jnp.where(
                        half8,
                        rim_cols[p * 8 : p * 8 + 8, 72 * side + 8 * way(dx, -1) + r : 72 * side + 8 * way(dx, -1) + r + 1],
                        rim_cols[p * 8 : p * 8 + 8, 72 * side + 8 * way(dx, 1) + r : 72 * side + 8 * way(dx, 1) + r + 1],
                    )
                ],
                axis=0,
            )
            volp[tap * 40 : tap * 40 + 40, lanes] = jnp.where(
                lane40 == lane, jnp.broadcast_to(col, (40, 128)), pltpu.roll(plane, turn, 1)
            )

    y_of = const("y_of").astype(F32)
    sums = []
    for a in range(3):
        g = nt(delta, volp[:, a * 128 : (a + 4) * 128].astype(BF16))
        for b in range(3):
            total = jnp.zeros((16, 128), F32)
            for y in range(8):
                total = total + jnp.where(y_of == y + b, g[y * 16 : y * 16 + 16], 0.0)
            sums.append(total)
    sums = jnp.concatenate(sums, axis=1)
    top = sums.astype(BF16)
    rest = (sums - top.astype(F32)).astype(BF16)
    fold = const("fold")
    packed = nn(top, fold) + nn(rest, fold)

    def fold_y(v):
        out = v[0:16]
        for y in range(1, 8):
            out = out + v[y * 16 : y * 16 + 16]
        return jnp.broadcast_to(jnp.sum(out, axis=1, keepdims=True), (16, 128))

    lane16 = lax.broadcasted_iota(jnp.int32, (16, 128), 1)
    share[64:80] = jnp.where(lane16 >= 108, fold_y(bias_one), packed)
    share[80:96] = jnp.zeros((16, 128), F32)

    slot = lax.shift_right_logical(lane16, 4)
    blocks = [jnp.zeros((16, 128), F32) for _ in range(4)]
    for a in range(3):
        g = nt(planes[0:480, (2 - a) * 128 : (6 - a) * 128], acts[...])
        for b in range(3):
            for c in range(3):
                t = (a * 3 + b) * 3 + c
                total = jnp.zeros((16, 128), F32)
                for y in range(8):
                    at = c * 160 + (y + 2 - b) * 16
                    total = jnp.where(slot == y, g[at : at + 16], total)
                for turn in (64, 32, 16):
                    total = total + pltpu.roll(total, turn, 1)
                blocks[t // 8] = jnp.where(slot == t % 8, total, blocks[t // 8])
    blocks[3] = jnp.where(slot == 3, fold_y(bias_two), blocks[3])
    for k in range(4):
        share[k * 16 : k * 16 + 16] = blocks[k]

    def scatter(k, _):
        t, where = in_group(k)
        pltpu.make_async_remote_copy(
            share.at[pl.ds(ROWS * t, ROWS)], got1.at[pl.ds(4 * group_at, ROWS)],
            red_send.at[0], red_recv.at[0], device_id=where, device_id_type=MESH,
        ).start()
        return 0

    lax.fori_loop(1, n_group, scatter, 0)
    own = pltpu.make_async_copy(share.at[pl.ds(ROWS * group_at, ROWS)], got1.at[pl.ds(4 * group_at, ROWS)], own_sem.at[0])
    own.start()
    own.wait()

    def await_rows(sem, ref, n):
        ref = ref.at[pl.ds(0, n * ROWS)]
        pltpu.make_async_copy(ref, ref, sem).wait()

    def total8(ref, n):
        out = ref[0:8]
        for i in range(1, n // 2):
            out = out + ref[i * 8 : i * 8 + 8]
        return out + pltpu.roll(out, 4, 0)

    await_rows(red_recv.at[0], got1, n_group - 1)
    mid1[...] = total8(got1, n_group)

    def along(k, _):
        _, where = in_line(k)
        pltpu.make_async_remote_copy(
            mid1.at[pl.ds(0, ROWS)], got2.at[pl.ds(4 * line_at, ROWS)],
            red_send.at[1], red_recv.at[1], device_id=where, device_id_type=MESH,
        ).start()
        return 0

    lax.fori_loop(1, n_line, along, 0)
    own = pltpu.make_async_copy(mid1.at[pl.ds(0, ROWS)], got2.at[pl.ds(4 * line_at, ROWS)], own_sem.at[1])
    own.start()
    own.wait()

    settle(recv_sem, 1, xr2, yr2, xyr2, zr2)
    build_planes(1, lambda x: inner[x], xr2, yr2, xyr2, zr2)
    grad = nn(m_one[0], planes[:, 256:768]) + nn(m_one[1], planes[:, 128:640]) + nn(m_one[2], planes[:, 0:512])
    for j in range(4):
        for x in range(4):
            gvol[j, x] = grad[j * 8 : j * 8 + 8, x * 128 : (x + 1) * 128]

    await_rows(red_recv.at[1], got2, n_line - 1)
    mid2[...] = total8(got2, n_line) * norm

    def gather(k, _):
        _, where = in_group(k)
        pltpu.make_async_remote_copy(
            mid2.at[pl.ds(0, ROWS)], summed.at[pl.ds(ROWS * group_at, ROWS)],
            red_send.at[2], red_recv.at[2], device_id=where, device_id_type=MESH,
        ).start()
        return 0

    lax.fori_loop(1, n_group, gather, 0)
    own = pltpu.make_async_copy(mid2.at[pl.ds(0, ROWS)], summed.at[pl.ds(ROWS * group_at, ROWS)], own_sem.at[2])
    own.start()
    own.wait()
    settle(send_sem, 0, xr, yr, xyr, zr)
    settle(send_sem, 1, xr2, yr2, xyr2, zr2)
    await_rows(red_send.at[0], got1, n_group - 1)
    await_rows(red_send.at[1], got2, n_line - 1)
    await_rows(red_recv.at[2], summed, n_group - 1)

    for k in range(4):
        block = summed[k * 16 : k * 16 + 16]
        for s in range(8):
            if k * 8 + s < 27:
                turned = pltpu.roll(block, (128 - 16 * s) % 128, 1) if s else block
                gw2[k * 8 + s] = turned[:, 0:16]
    gb2[...] = summed[48:64].T[48:49, :]
    packed = summed[64:80].T
    for t in range(27):
        gw1[t] = packed[4 * t : 4 * t + 4, :]
    gb1[...] = packed[108:109, :]
    await_rows(red_send.at[2], summed, n_group - 1)


def local(sizes, norm, volume, act_one, act_two, weight_one, weight_two, cotangent):
    narrow, wide = constants()
    w1 = jnp.transpose(weight_one, (2, 3, 4, 1, 0)).reshape(27, CHAN_IN, CHAN)
    w2 = jnp.transpose(weight_two, (2, 3, 4, 0, 1)).reshape(27, CHAN, CHAN)
    n_group = sizes[0] * 4
    n_line = sizes[1] * (sizes[2] // 4)
    buf = lambda *shape: pltpu.VMEM(shape, BF16)
    buf32 = lambda *shape: pltpu.VMEM(shape, F32)
    block = (CHAN, NX, NY, NZ)
    gw1, gb1, gw2, gb2, gvol = pl.pallas_call(
        functools.partial(kernel, sizes, norm),
        out_shape=(
            jax.ShapeDtypeStruct((27, CHAN_IN, CHAN), F32),
            jax.ShapeDtypeStruct((1, CHAN), F32),
            jax.ShapeDtypeStruct((27, CHAN, CHAN), F32),
            jax.ShapeDtypeStruct((1, CHAN), F32),
            jax.ShapeDtypeStruct((CHAN_IN, NX, NY, NZ), F32),
        ),
        in_specs=[pl.BlockSpec(memory_space=pl.ANY)] * 8,
        out_specs=tuple([pl.BlockSpec(memory_space=pltpu.VMEM)] * 5),
        scratch_shapes=[
            buf(CHAN_IN, NX, NY, NZ), buf(*block), buf(*block), buf(27, CHAN_IN, CHAN), buf(27, CHAN, CHAN), buf(*block),
            buf(NARROW, 128), buf(208, 512),
            buf(2, 160, 128), buf(2, 160, 128), buf(2, 80, 128), buf(2, 80, 128), buf(4, 32, 128), buf32(2, 8, 128), buf32(2, 72, 128),
            buf(2, 128, 128), buf(2, 128, 128), buf(2, 64, 128), buf(2, 64, 128), buf(4, 16, 128), buf32(2, 8, 128), buf32(2, 72, 128),
            buf(4, 128, 128), buf(128, 512), buf(512, 768), buf32(128, 768), buf(3, 128, 512), buf(3, 32, 512),
            buf32(96, 128), buf32(4 * n_group, 128), buf32(4 * n_line, 128), buf32(8, 128), buf32(8, 128), buf32(96, 128),
            pltpu.SemaphoreType.DMA((8,)), pltpu.SemaphoreType.DMA((3,)),
            pltpu.SemaphoreType.DMA((2, 4)), pltpu.SemaphoreType.DMA((2, 4)),
            pltpu.SemaphoreType.DMA((3,)), pltpu.SemaphoreType.DMA((3,)),
        ],
        compiler_params=pltpu.CompilerParams(collective_id=0, has_side_effects=True),
        name="both_layers",
    )(volume, act_one, act_two, w1, w2, cotangent, narrow, wide)
    gw1 = jnp.transpose(gw1.reshape(3, 3, 3, CHAN_IN, CHAN), (4, 3, 0, 1, 2))
    gw2 = jnp.transpose(gw2.reshape(3, 3, 3, CHAN, CHAN), (3, 4, 0, 1, 2))
    return gw1, gb1.reshape(CHAN), gw2, gb2.reshape(CHAN), gvol


def solution(mesh):
    sizes = tuple(mesh.shape[name] for name in ("gx", "gy", "gz"))
    norm = 1.0 / math.sqrt(NX * NY * NZ * sizes[0] * sizes[1] * sizes[2])
    block = P(None, "gx", "gy", "gz")
    return jax.shard_map(
        functools.partial(local, sizes, norm),
        mesh=mesh,
        in_specs=(block, block, block, P(), P(), block),
        out_specs=(P(), P(), P(), P(), block),
        check_vma=False,
    )
```

time: 255 us -> 53.7 us (0.21)
  blocking collectives: 118 us -> 0 us
  starting transfers between devices: 73.6 us -> 0 us
  Pallas kernels: 0 us -> 48.1 us
  waiting for transfers between devices: 24.3 us -> 0 us
  matrix products: 20.9 us -> 0 us
  local copies, waits for them, and re-layouts: 12.8 us -> 4.77 us
  other arithmetic: 3.72 us -> 0 us
    psum x1 -> x0, blocking collectives: 118 us -> none  [packed_total(): subtotal = lax.psum(jnp.concatenate([a.ravel() for a in arrays]), axis)]
    ppermute x12 -> x0, starting transfers between devices: 73.6 us -> none  [the longest x6 59.3 us: with_halo(): lax.ppermute(head, axis, [((i + 1) % count, i) for i in range(count)])]
    pallas_call x0 -> x1, Pallas kernels: none -> 48.1 us  [local(): pl.pallas_call(functools.partial(kernel, sizes, norm), out_shape=(jax.Sha...]
    ppermute x12 -> x0, waiting for transfers between devices: 24.3 us -> none  [the longest x6 19.5 us: with_halo(): lax.ppermute(tail, axis, [(i, (i + 1) % count) for i in range(count)])]
    dot_general x108 -> x0, matrix products: 20.9 us -> none  [the longest x54 10.6 us: weight_from_deltas(): jnp.einsum('oc,ic->oi', shifted, flat_source, preferred_element_type=jnp....]
    slice x62 -> x0, local copies, waits for them, and re-layouts: 6.77 us -> none  [the longest x58 6.49 us: window(): lax.slice(padded, (0, start_x, start_y, start_z), (depth, start_x + exten...]
  transfers between devices with their start and end apart: 12 -> 0, of which waited for: 9 -> 0; matrix products, arithmetic and copies ran while one was open for 2% -> 0% of each run, Pallas kernels for 0% -> 0%
where the time goes in v1:
time: 53.7 us; the launch traced here: 53.5 us
  Pallas kernels  48.1 us (90%)
  local copies, waits for them, and re-layouts  4.77 us (9%)
  between operations  0.65 us (1%)
    pallas_call x1, Pallas kernels, local(): pl.pallas_call(functools.partial(kernel, sizes, norm), out_shape=(jax.Sha...  48.1 us
    unnamed x11, local copies, waits for them, and re-layouts  4.77 us

profile of v1, /device:TPU:1, one launch (start us, length us, event | category | flops | bytes accessed | tf_op | source)
XLA Modules:
  0.0 53.5 jit_solution(13736176461442918902)
XLA Ops:
  0.6 48.1 %both_layers.1 = (f32[27,4,16]{2,1,0:T(4,128)}, f32[1,16]{1,0:T(1,128)}, f32[27,16,16]{2,1,0:T(8,128)}, f32[1,16]{1,0:T(1,128)}, f32[4,4,8,128]{3,2,1,0:T(8,128)}) custom-call(bf16[4,4,8,128]{3,2,1,0:T(8,128)(2,1)} %vol_h.1, bf16[16,4,8,128]{3,2,1,0:T(8,128)(2,1)} %act1_h.1, bf16[16,4,8,128]{3,2,1,0:T(8,128)(2,1)} %act2_h.1, bf16[27,4,16]{2,1,0:T(4,128)(2,1)} %bitcast.17, ...), custom_call_target="tpu_custom_call" | custom-call | tf_op jit(solution)/shard_map/both_layers/pallas_call | solution.py:513
  48.7 0.0 copy-start.2
  48.7 1.4 %copy.18 = f32[16,4,3,3,3]{0,1,4,3,2:T(4,128)} copy(f32[16,4,3,3,3]{0,1,4,3,2:T(4,128)} %bitcast.16) | data formatting | bytes 13824
  50.2 0.0 copy-done.2
  50.2 0.5 copy.19
  50.7 0.0 copy-start.1
  50.7 0.0 copy-start
  50.7 1.7 %copy.20 = f32[16,16,3,3,3]{1,0,4,3,2:T(8,128)} copy(f32[16,16,3,3,3]{1,0,4,3,2:T(8,128)} %bitcast.14) | data formatting | bytes 55296
  52.3 0.0 copy-done.1
  52.3 0.5 copy.21
  52.9 0.0 copy-done
  52.9 0.6 %copy.22 = f32[4,4,8,128]{3,2,1,0:T(8,128)} copy(f32[4,4,8,128]{3,2,1,0:T(8,128)S(1)} %copy-done) | data formatting | bytes 131072
Async XLA Ops:
  48.7 1.5 %copy-start.2 = (f32[1,16]{1,0:T(1,128)S(1)}, f32[1,16]{1,0:T(1,128)}, u32[]{:S(2)}) copy-start(f32[1,16]{1,0:T(1,128)} %get-tuple-element.11) | copy-start | bytes 196
  50.7 1.7 %copy-start.1 = (f32[1,16]{1,0:T(1,128)S(1)}, f32[1,16]{1,0:T(1,128)}, u32[]{:S(2)}) copy-start(f32[1,16]{1,0:T(1,128)} %get-tuple-element.13) | copy-start | bytes 196
  50.7 2.2 %copy-start = (f32[4,4,8,128]{3,2,1,0:T(8,128)S(1)}, f32[4,4,8,128]{3,2,1,0:T(8,128)}, u32[]{:S(2)}) copy-start(f32[4,4,8,128]{3,2,1,0:T(8,128)} %get-tuple-element.24) | copy-start | bytes 196612

commit v2 on v1

--- a/solution.py
+++ b/solution.py
@@ -95,11 +95,11 @@
 def kernel(
     sizes, norm,
     vol_h, act1_h, act2_h, w1_h, w2_h, cot_h, narrow_h, wide_h,
-    gw1, gb1, gw2, gb2, gvol,
+    summed, gvol,
     vol_v, act1_v, act2_v, w1_v, w2_v, cot_v, narrow_v, wide_v,
     xs, xr, ys, yr, xyr, zs, zr,
     xs2, xr2, ys2, yr2, xyr2, zs2, zr2,
-    inner, acts, planes, volp, m_two, m_one, share, got1, got2, mid1, mid2, summed,
+    inner, acts, planes, volp, m_two, m_one, share, got1, got2, mid1, mid2,
     load_sem, own_sem, send_sem, recv_sem, red_send, red_recv,
 ):
     n_gx, n_gy, n_gz = sizes
@@ -487,18 +487,35 @@
     await_rows(red_send.at[1], got2, n_line - 1)
     await_rows(red_recv.at[2], summed, n_group - 1)
 
+    await_rows(red_send.at[2], summed, n_group - 1)
+
+
+def finish(
+    summed, gvol_v, gw1, gb1, gw2, gb2, gvol,
+    gw1_v, gb1_v, gw2_v, gb2_v, sems,
+):
+    copies = [
+        pltpu.make_async_copy(src, dst, sems.at[i])
+        for i, (src, dst) in enumerate(((gvol_v, gvol), (gw2_v, gw2), (gw1_v, gw1), (gb1_v, gb1), (gb2_v, gb2)))
+    ]
+    copies[0].start()
     for k in range(4):
         block = summed[k * 16 : k * 16 + 16]
         for s in range(8):
             if k * 8 + s < 27:
                 turned = pltpu.roll(block, (128 - 16 * s) % 128, 1) if s else block
-                gw2[k * 8 + s] = turned[:, 0:16]
-    gb2[...] = summed[48:64].T[48:49, :]
+                gw2_v[k * 8 + s] = turned[:, 0:16]
+    copies[1].start()
     packed = summed[64:80].T
     for t in range(27):
-        gw1[t] = packed[4 * t : 4 * t + 4, :]
-    gb1[...] = packed[108:109, :]
-    await_rows(red_send.at[2], summed, n_group - 1)
+        gw1_v[t] = packed[4 * t : 4 * t + 4, :]
+    copies[2].start()
+    gb1_v[...] = packed[108, :]
+    gb2_v[...] = summed[48:64].T[48, :]
+    copies[3].start()
+    copies[4].start()
+    for copy in copies:
+        copy.wait()
 
 
 def local(sizes, norm, volume, act_one, act_two, weight_one, weight_two, cotangent):
@@ -510,34 +527,41 @@
     buf = lambda *shape: pltpu.VMEM(shape, BF16)
     buf32 = lambda *shape: pltpu.VMEM(shape, F32)
     block = (CHAN, NX, NY, NZ)
-    gw1, gb1, gw2, gb2, gvol = pl.pallas_call(
+    summed, gvol = pl.pallas_call(
         functools.partial(kernel, sizes, norm),
         out_shape=(
-            jax.ShapeDtypeStruct((27, CHAN_IN, CHAN), F32),
-            jax.ShapeDtypeStruct((1, CHAN), F32),
-            jax.ShapeDtypeStruct((27, CHAN, CHAN), F32),
-            jax.ShapeDtypeStruct((1, CHAN), F32),
-            jax.ShapeDtypeStruct((CHAN_IN, NX, NY, NZ), F32),
+            pltpu.VMEM((96, 128), F32),
+            pltpu.VMEM((CHAN_IN, NX, NY, NZ), F32),
         ),
         in_specs=[pl.BlockSpec(memory_space=pl.ANY)] * 8,
-        out_specs=tuple([pl.BlockSpec(memory_space=pltpu.VMEM)] * 5),
+        out_specs=tuple([pl.BlockSpec(memory_space=pltpu.VMEM)] * 2),
         scratch_shapes=[
             buf(CHAN_IN, NX, NY, NZ), buf(*block), buf(*block), buf(27, CHAN_IN, CHAN), buf(27, CHAN, CHAN), buf(*block),
             buf(NARROW, 128), buf(208, 512),
             buf(2, 160, 128), buf(2, 160, 128), buf(2, 80, 128), buf(2, 80, 128), buf(4, 32, 128), buf32(2, 8, 128), buf32(2, 72, 128),
             buf(2, 128, 128), buf(2, 128, 128), buf(2, 64, 128), buf(2, 64, 128), buf(4, 16, 128), buf32(2, 8, 128), buf32(2, 72, 128),
             buf(4, 128, 128), buf(128, 512), buf(512, 768), buf32(128, 768), buf(3, 128, 512), buf(3, 32, 512),
-            buf32(96, 128), buf32(4 * n_group, 128), buf32(4 * n_line, 128), buf32(8, 128), buf32(8, 128), buf32(96, 128),
+            buf32(96, 128), buf32(4 * n_group, 128), buf32(4 * n_line, 128), buf32(8, 128), buf32(8, 128),
             pltpu.SemaphoreType.DMA((8,)), pltpu.SemaphoreType.DMA((3,)),
             pltpu.SemaphoreType.DMA((2, 4)), pltpu.SemaphoreType.DMA((2, 4)),
             pltpu.SemaphoreType.DMA((3,)), pltpu.SemaphoreType.DMA((3,)),
         ],
-        compiler_params=pltpu.CompilerParams(collective_id=0, has_side_effects=True),
+        compiler_params=pltpu.CompilerParams(collective_id=0, has_side_effects=True, vmem_limit_bytes=60 * 2**20),
         name="both_layers",
     )(volume, act_one, act_two, w1, w2, cotangent, narrow, wide)
+    shapes = ((27, CHAN_IN, CHAN), (CHAN,), (27, CHAN, CHAN), (CHAN,))
+    gw1, gb1, gw2, gb2, gvol = pl.pallas_call(
+        finish,
+        out_shape=tuple(jax.ShapeDtypeStruct(shape, F32) for shape in shapes + ((CHAN_IN, NX, NY, NZ),)),
+        in_specs=[pl.BlockSpec(memory_space=pltpu.VMEM)] * 2,
+        out_specs=tuple([pl.BlockSpec(memory_space=pl.ANY)] * 5),
+        scratch_shapes=[buf32(*shape) for shape in shapes] + [pltpu.SemaphoreType.DMA((5,))],
+        compiler_params=pltpu.CompilerParams(vmem_limit_bytes=8 * 2**20),
+        name="finish",
+    )(summed, gvol)
     gw1 = jnp.transpose(gw1.reshape(3, 3, 3, CHAN_IN, CHAN), (4, 3, 0, 1, 2))
     gw2 = jnp.transpose(gw2.reshape(3, 3, 3, CHAN, CHAN), (3, 4, 0, 1, 2))
-    return gw1, gb1.reshape(CHAN), gw2, gb2.reshape(CHAN), gvol
+    return gw1, gb1, gw2, gb2, gvol
 
 
 def solution(mesh):

time: 53.7 us -> 48.8 us (0.909)
  local copies, waits for them, and re-layouts: 4.77 us -> 0 us
    unnamed x11 -> x0, local copies, waits for them, and re-layouts: 4.77 us -> none
    pallas_call x1 -> x2, Pallas kernels: 48.1 us -> 48 us  [the longest x1 47.1 us: local(): pl.pallas_call(functools.partial(kernel, sizes, norm), out_shape=(pltpu.V...]
where the time goes in v2:
time: 48.8 us; the launch traced here: 48.6 us
  Pallas kernels  48 us (98%)
  between operations  0.64 us (1%)
    pallas_call x1, Pallas kernels, local(): pl.pallas_call(functools.partial(kernel, sizes, norm), out_shape=(pltpu.V...  47.1 us

profile of v2, /device:TPU:1, one launch (start us, length us, event | category | flops | bytes accessed | tf_op | source)
XLA Modules:
  0.0 48.6 jit_solution(15887863270615972901)
XLA Ops:
  0.6 47.1 %both_layers.1 = (f32[96,128]{1,0:T(8,128)S(1)}, f32[4,4,8,128]{3,2,1,0:T(8,128)S(1)}) custom-call(bf16[4,4,8,128]{3,2,1,0:T(8,128)(2,1)} %vol_h.1, bf16[16,4,8,128]{3,2,1,0:T(8,128)(2,1)} %act1_h.1, bf16[16,4,8,128]{3,2,1,0:T(8,128)(2,1)} %act2_h.1, bf16[27,4,16]{2,1,0:T(4,128)(2,1)} %bitcast.13, bf16[27,16,16]{2,1,0:T(8,128)(2,1)} %bitcast.12, ...), custom_call_target="tpu_custom_call" | custom-call | tf_op jit(solution)/shard_map/both_layers/pallas_call | solution.py:530
  47.8 0.9 %finish.1 = (f32[27,4,16]{2,1,0:T(4,128)}, f32[16]{0:T(128)}, f32[27,16,16]{2,1,0:T(8,128)}, f32[16]{0:T(128)}, f32[4,4,8,128]{3,2,1,0:T(8,128)}) custom-call(f32[96,128]{1,0:T(8,128)S(1)} %get-tuple-element.12.summed, f32[4,4,8,128]{3,2,1,0:T(8,128)S(1)} %get-tuple-element.13.gvol_v), custom_call_target="tpu_custom_call" | custom-call | tf_op jit(solution)/shard_map/finish/pallas_call | solution.py:553

commit v3 on v2

--- a/solution.py
+++ b/solution.py
@@ -64,13 +64,13 @@
     for ab in range(9):
         for q in range(120):
             fold[ab, q, (ab * 3 + row_c[q]) * 4 + row_j[q]] = 1
-    narrow = np.concatenate([narrow, y_of, fold.reshape(-1, 128)])
-    return jnp.asarray(narrow, BF16), jnp.asarray(wide, BF16)
+    narrow = np.concatenate([narrow, y_of])
+    return jnp.asarray(narrow, BF16), jnp.asarray(wide, BF16), jnp.asarray(fold.reshape(-1, 128), BF16)
 
 
 AT = {}
 _at = 0
-for _name, _n in (("perm", 128), ("eye", 128), ("ends", 16), ("tiles", 32), ("rim_cols", 48), ("rim_rows", 48), ("spread", 128), ("y_of", 16), ("fold", 1152)):
+for _name, _n in (("perm", 128), ("eye", 128), ("ends", 16), ("tiles", 32), ("rim_cols", 48), ("rim_rows", 48), ("spread", 128), ("y_of", 16)):
     AT[_name] = (_at, _n)
     _at += _n
 NARROW = _at
@@ -94,9 +94,9 @@
 
 def kernel(
     sizes, norm,
-    vol_h, act1_h, act2_h, w1_h, w2_h, cot_h, narrow_h, wide_h,
+    vol_h, act1_h, act2_h, w1_h, w2_h, cot_h, narrow_h, wide_h, fold_h,
     summed, gvol,
-    vol_v, act1_v, act2_v, w1_v, w2_v, cot_v, narrow_v, wide_v,
+    vol_v, act1_v, act2_v, w1_v, w2_v, cot_v, narrow_v, wide_v, fold_v,
     xs, xr, ys, yr, xyr, zs, zr,
     xs2, xr2, ys2, yr2, xyr2, zs2, zr2,
     inner, acts, planes, volp, m_two, m_one, share, got1, got2, mid1, mid2,
@@ -112,20 +112,40 @@
     group_at = gx * n_y + y_pos
     line_at = hi_pos * n_gy + gy
 
+    loads = [
+        pltpu.make_async_copy(src, dst, load_sem.at[i])
+        for i, (src, dst) in enumerate(
+            ((cot_h, cot_v), (act2_h, act2_v), (narrow_h, narrow_v), (vol_h, vol_v), (act1_h, act1_v), (wide_h, wide_v), (w2_h, w2_v), (w1_h, w1_v), (fold_h, fold_v))
+        )
+    ]
+    for copy in loads[:4]:
+        copy.start()
+
+    gx_at = [lax.rem(gx + d, n_gx) for d in range(n_gx)]
+    gy_at = [lax.rem(gy + d, n_gy) for d in range(n_gy)]
+    gz_at = [lax.rem(gz + d, n_gz) for d in range(n_gz)]
+    y_at = [lax.rem(y_pos + d, n_y) for d in range(n_y)]
+    line_to = [lax.rem(line_at + d, n_line) for d in range(n_line)]
+    run_base = hi_pos * n_y
+
     def near(dx, dy, dz):
-        return (
-            lax.rem(gx + (n_gx + dx), n_gx),
-            lax.rem(gy + (n_gy + dy), n_gy),
-            lax.rem(gz + (n_gz + dz), n_gz),
-        )
-
-    def in_group(k):
-        t = lax.rem(group_at + k, n_group)
-        return t, (lax.div(t, n_y), gy, hi_pos * n_y + lax.rem(t, n_y))
-
-    def in_line(k):
-        t = lax.rem(line_at + k, n_line)
-        return t, (gx, lax.rem(t, n_gy), lax.div(t, n_gy) * n_y + y_pos)
+        return gx_at[dx], gy_at[dy], gz_at[dz]
+
+    def ring(d, n):
+        return min(d, n - d)
+
+    group_steps = sorted(
+        ((d, e) for d in range(n_gx) for e in range(n_y) if (d, e) != (0, 0)),
+        key=lambda p: -(ring(p[0], n_gx) / 2 + ring(p[1], n_y)),
+    )
+    line_steps = sorted(range(1, n_line), key=lambda d: -ring(d, n_line))
+
+    def in_group(step):
+        d, e = step
+        return gx_at[d] * n_y + y_at[e], (gx_at[d], gy, run_base + y_at[e])
+
+    def in_line(d):
+        return gx, lax.rem(line_to[d], n_gy), lax.div(line_to[d], n_gy) * n_y + y_pos
 
     barrier = pltpu.get_barrier_semaphore()
     for dz in (-1, 1, 0):
@@ -134,24 +154,11 @@
                 if (dx, dy, dz) != (0, 0, 0):
                     pl.semaphore_signal(barrier, inc=1, device_id=near(dx, dy, dz), device_id_type=MESH)
 
-    def greet_line(k, _):
-        pl.semaphore_signal(barrier, inc=1, device_id=in_line(k)[1], device_id_type=MESH)
-        return 0
-
-    def greet_group(k, _):
-        pl.semaphore_signal(barrier, inc=1, device_id=in_group(k)[1], device_id_type=MESH)
-        return 0
-
-    lax.fori_loop(1, n_line, greet_line, 0)
-    lax.fori_loop(1, n_group, greet_group, 0)
-
-    loads = [
-        pltpu.make_async_copy(src, dst, load_sem.at[i])
-        for i, (src, dst) in enumerate(
-            ((cot_h, cot_v), (act2_h, act2_v), (narrow_h, narrow_v), (vol_h, vol_v), (act1_h, act1_v), (wide_h, wide_v), (w2_h, w2_v), (w1_h, w1_v))
-        )
-    ]
-    for copy in loads:
+    for d in line_steps:
+        pl.semaphore_signal(barrier, inc=1, device_id=in_line(d), device_id_type=MESH)
+    for step in group_steps:
+        pl.semaphore_signal(barrier, inc=1, device_id=in_group(step)[1], device_id_type=MESH)
+    for copy in loads[4:]:
         copy.start()
 
     def const(name):
@@ -292,7 +299,7 @@
 
     exchange(0, xs, xr, ys, yr, xyr, zs, zr)
 
-    for i in range(4, 8):
+    for i in range(4, 9):
         loads[i].wait()
     turned = nn(perm, jnp.concatenate([rows_of(act1_v, x).astype(BF16) for x in range(4)], axis=1))
     acts[...] = turned.astype(BF16)
@@ -389,7 +396,7 @@
     sums = jnp.concatenate(sums, axis=1)
     top = sums.astype(BF16)
     rest = (sums - top.astype(F32)).astype(BF16)
-    fold = const("fold")
+    fold = fold_v[...]
     packed = nn(top, fold) + nn(rest, fold)
 
     def fold_y(v):
@@ -420,15 +427,12 @@
     for k in range(4):
         share[k * 16 : k * 16 + 16] = blocks[k]
 
-    def scatter(k, _):
-        t, where = in_group(k)
+    for step in group_steps:
+        t, where = in_group(step)
         pltpu.make_async_remote_copy(
             share.at[pl.ds(ROWS * t, ROWS)], got1.at[pl.ds(4 * group_at, ROWS)],
             red_send.at[0], red_recv.at[0], device_id=where, device_id_type=MESH,
         ).start()
-        return 0
-
-    lax.fori_loop(1, n_group, scatter, 0)
     own = pltpu.make_async_copy(share.at[pl.ds(ROWS * group_at, ROWS)], got1.at[pl.ds(4 * group_at, ROWS)], own_sem.at[0])
     own.start()
     own.wait()
@@ -446,15 +450,11 @@
     await_rows(red_recv.at[0], got1, n_group - 1)
     mid1[...] = total8(got1, n_group)
 
-    def along(k, _):
-        _, where = in_line(k)
+    for d in line_steps:
         pltpu.make_async_remote_copy(
             mid1.at[pl.ds(0, ROWS)], got2.at[pl.ds(4 * line_at, ROWS)],
-            red_send.at[1], red_recv.at[1], device_id=where, device_id_type=MESH,
+            red_send.at[1], red_recv.at[1], device_id=in_line(d), device_id_type=MESH,
         ).start()
-        return 0
-
-    lax.fori_loop(1, n_line, along, 0)
     own = pltpu.make_async_copy(mid1.at[pl.ds(0, ROWS)], got2.at[pl.ds(4 * line_at, ROWS)], own_sem.at[1])
     own.start()
     own.wait()
@@ -469,15 +469,11 @@
     await_rows(red_recv.at[1], got2, n_line - 1)
     mid2[...] = total8(got2, n_line) * norm
 
-    def gather(k, _):
-        _, where = in_group(k)
+    for step in group_steps:
         pltpu.make_async_remote_copy(
             mid2.at[pl.ds(0, ROWS)], summed.at[pl.ds(ROWS * group_at, ROWS)],
-            red_send.at[2], red_recv.at[2], device_id=where, device_id_type=MESH,
+            red_send.at[2], red_recv.at[2], device_id=in_group(step)[1], device_id_type=MESH,
         ).start()
-        return 0
-
-    lax.fori_loop(1, n_group, gather, 0)
     own = pltpu.make_async_copy(mid2.at[pl.ds(0, ROWS)], summed.at[pl.ds(ROWS * group_at, ROWS)], own_sem.at[2])
     own.start()
     own.wait()
@@ -519,7 +515,7 @@
 
 
 def local(sizes, norm, volume, act_one, act_two, weight_one, weight_two, cotangent):
-    narrow, wide = constants()
+    narrow, wide, fold = constants()
     w1 = jnp.transpose(weight_one, (2, 3, 4, 1, 0)).reshape(27, CHAN_IN, CHAN)
     w2 = jnp.transpose(weight_two, (2, 3, 4, 0, 1)).reshape(27, CHAN, CHAN)
     n_group = sizes[0] * 4
@@ -533,22 +529,22 @@
             pltpu.VMEM((96, 128), F32),
             pltpu.VMEM((CHAN_IN, NX, NY, NZ), F32),
         ),
-        in_specs=[pl.BlockSpec(memory_space=pl.ANY)] * 8,
+        in_specs=[pl.BlockSpec(memory_space=pl.ANY)] * 9,
         out_specs=tuple([pl.BlockSpec(memory_space=pltpu.VMEM)] * 2),
         scratch_shapes=[
             buf(CHAN_IN, NX, NY, NZ), buf(*block), buf(*block), buf(27, CHAN_IN, CHAN), buf(27, CHAN, CHAN), buf(*block),
-            buf(NARROW, 128), buf(208, 512),
+            buf(NARROW, 128), buf(208, 512), buf(1152, 128),
             buf(2, 160, 128), buf(2, 160, 128), buf(2, 80, 128), buf(2, 80, 128), buf(4, 32, 128), buf32(2, 8, 128), buf32(2, 72, 128),
             buf(2, 128, 128), buf(2, 128, 128), buf(2, 64, 128), buf(2, 64, 128), buf(4, 16, 128), buf32(2, 8, 128), buf32(2, 72, 128),
             buf(4, 128, 128), buf(128, 512), buf(512, 768), buf32(128, 768), buf(3, 128, 512), buf(3, 32, 512),
             buf32(96, 128), buf32(4 * n_group, 128), buf32(4 * n_line, 128), buf32(8, 128), buf32(8, 128),
-            pltpu.SemaphoreType.DMA((8,)), pltpu.SemaphoreType.DMA((3,)),
+            pltpu.SemaphoreType.DMA((9,)), pltpu.SemaphoreType.DMA((3,)),
             pltpu.SemaphoreType.DMA((2, 4)), pltpu.SemaphoreType.DMA((2, 4)),
             pltpu.SemaphoreType.DMA((3,)), pltpu.SemaphoreType.DMA((3,)),
         ],
         compiler_params=pltpu.CompilerParams(collective_id=0, has_side_effects=True, vmem_limit_bytes=60 * 2**20),
         name="both_layers",
-    )(volume, act_one, act_two, w1, w2, cotangent, narrow, wide)
+    )(volume, act_one, act_two, w1, w2, cotangent, narrow, wide, fold)
     shapes = ((27, CHAN_IN, CHAN), (CHAN,), (27, CHAN, CHAN), (CHAN,))
     gw1, gb1, gw2, gb2, gvol = pl.pallas_call(
         finish,

time: 48.8 us -> 48.4 us (level)
  no operation moved by 1% of the time
where the time goes in v3:
time: 48.4 us; the launch traced here: 48.2 us
  Pallas kernels  47.6 us (98%)
  between operations  0.64 us (1%)
    pallas_call x1, Pallas kernels, local(): pl.pallas_call(functools.partial(kernel, sizes, norm), out_shape=(pltpu.V...  46.7 us

profile of v3, /device:TPU:1, one launch (start us, length us, event | category | flops | bytes accessed | tf_op | source)
XLA Modules:
  0.0 48.2 jit_solution(2651639061283607362)
XLA Ops:
  0.6 46.7 %both_layers.1 = (f32[96,128]{1,0:T(8,128)S(1)}, f32[4,4,8,128]{3,2,1,0:T(8,128)S(1)}) custom-call(bf16[4,4,8,128]{3,2,1,0:T(8,128)(2,1)} %vol_h.1, bf16[16,4,8,128]{3,2,1,0:T(8,128)(2,1)} %act1_h.1, bf16[16,4,8,128]{3,2,1,0:T(8,128)(2,1)} %act2_h.1, bf16[27,4,16]{2,1,0:T(4,128)(2,1)} %bitcast.13, bf16[27,16,16]{2,1,0:T(8,128)(2,1)} %bitcast.12, ...), custom_call_target="tpu_custom_call" | custom-call | tf_op jit(solution)/shard_map/both_layers/pallas_call | solution.py:526
  47.4 0.9 %finish.1 = (f32[27,4,16]{2,1,0:T(4,128)}, f32[16]{0:T(128)}, f32[27,16,16]{2,1,0:T(8,128)}, f32[16]{0:T(128)}, f32[4,4,8,128]{3,2,1,0:T(8,128)}) custom-call(f32[96,128]{1,0:T(8,128)S(1)} %get-tuple-element.12.summed, f32[4,4,8,128]{3,2,1,0:T(8,128)S(1)} %get-tuple-element.13.gvol_v), custom_call_target="tpu_custom_call" | custom-call | tf_op jit(solution)/shard_map/finish/pallas_call | solution.py:549

commit v4 on v3

--- a/solution.py
+++ b/solution.py
@@ -99,7 +99,7 @@
     vol_v, act1_v, act2_v, w1_v, w2_v, cot_v, narrow_v, wide_v, fold_v,
     xs, xr, ys, yr, xyr, zs, zr,
     xs2, xr2, ys2, yr2, xyr2, zs2, zr2,
-    inner, acts, planes, volp, m_two, m_one, share, got1, got2, mid1, mid2,
+    inner, acts, planes, rotated, volp, m_two, m_one, share, got1, got2, mid1, mid2,
     load_sem, own_sem, send_sem, recv_sem, red_send, red_recv,
 ):
     n_gx, n_gy, n_gz = sizes
@@ -250,24 +250,44 @@
                     at, n = (0 if dx == -1 else 16), 16
                 send(3, ys.at[(dy + 1) // 2, pl.ds(at, n)], xyr.at[corner(-dx, -dy)], near(dx, dy, 0))
 
-    def settle(sems, phase, xr, yr, xyr, zr):
-        n = 42 if phase == 0 else 24
-        for kind, ref in ((0, zr.at[0, pl.ds(0, n)]), (1, xr), (2, yr), (3, xyr)):
-            pltpu.make_async_copy(ref, ref, sems.at[phase, kind]).wait()
+    def settle(sems, phase, kinds, xr, yr, xyr, zr):
+        refs = (zr.at[0, pl.ds(0, 42 if phase == 0 else 24)], xr, yr, xyr)
+        for kind in kinds:
+            pltpu.make_async_copy(refs[kind], refs[kind], sems.at[phase, kind]).wait()
 
     lane_of = lax.broadcasted_iota(jnp.int32, (160, 128), 1)
 
-    def build_planes(phase, inner_at, xr, yr, xyr, zr):
+    TURNS = ((0, 1, 127, 127), (2, 0, 1, 0))
+
+    def build_planes(phase, inner_at, xr, yr, xyr):
         first = phase == 0
-        cols = nt(eye, zr[...].reshape(144, 128).astype(BF16))
         tile_at = {0: 0, 3: 2, 1: 3, 2: 4} if first else {0: 0, 3: 1, 1: 2, 2: 3}
-        face_at = {0: 2, 3: 4, 1: 0, 2: 1} if first else {0: 2, 3: 3, 1: 0, 2: 1}
         for p in range(6):
             if 1 <= p <= 4:
                 x = p - 1
                 low = yr[0, tile_at[x] * 16 : tile_at[x] * 16 + 16]
                 mid = inner_at(x)
                 high = yr[1, tile_at[x] * 16 : tile_at[x] * 16 + 16]
+            else:
+                dx = -1 if p == 0 else 1
+                at = (16 if dx == -1 else 0) if first else 0
+                low = xyr[corner(dx, -1), at : at + 16]
+                mid = xr[(dx + 1) // 2, 0:128]
+                high = xyr[corner(dx, 1), at : at + 16]
+            plane = jnp.concatenate([low, mid, high], axis=0)
+            lanes = slice(p * 128, (p + 1) * 128)
+            planes[160:320, lanes] = plane
+            plane = plane.astype(F32)
+            for tap, side, turn, lane in TURNS:
+                rotated[side, :, lanes] = pltpu.roll(plane, turn, 1)
+
+    def close_planes(phase, zr):
+        first = phase == 0
+        cols = nt(eye, zr[...].reshape(144, 128).astype(BF16))
+        face_at = {0: 2, 3: 4, 1: 0, 2: 1} if first else {0: 2, 3: 3, 1: 0, 2: 1}
+        for p in range(6):
+            if 1 <= p <= 4:
+                x = p - 1
                 pick = (
                     (64 + 16 * x, 80 + 16 * x, 8 * way(0, -1)),
                     (0, 128, 8 * way(0, 0) + face_at[x]),
@@ -275,25 +295,18 @@
                 )
             else:
                 dx = -1 if p == 0 else 1
-                at = (16 if dx == -1 else 0) if first else 0
-                low = xyr[corner(dx, -1), at : at + 16]
-                mid = xr[(dx + 1) // 2, 0:128]
-                high = xyr[corner(dx, 1), at : at + 16]
                 r = (1 if dx == -1 else 0) if first else 0
                 pick = (
                     (112, 128, 8 * way(dx, -1) + r),
                     (0, 128, 8 * way(dx, 0) + r),
                     (0, 16, 8 * way(dx, 1) + r),
                 )
-            plane = jnp.concatenate([low, mid, high], axis=0)
             lanes = slice(p * 128, (p + 1) * 128)
-            planes[160:320, lanes] = plane
-            plane = plane.astype(F32)
-            for tap, side, turn, lane in ((0, 1, 127, 127), (2, 0, 1, 0)):
+            for tap, side, turn, lane in TURNS:
                 col = jnp.concatenate(
                     [cols[a:b, 72 * side + k : 72 * side + k + 1] for a, b, k in pick], axis=0
                 )
-                shifted = jnp.where(lane_of == lane, jnp.broadcast_to(col, (160, 128)), pltpu.roll(plane, turn, 1))
+                shifted = jnp.where(lane_of == lane, jnp.broadcast_to(col, (160, 128)), rotated[side, :, lanes])
                 planes[tap * 160 : tap * 160 + 160, lanes] = shifted.astype(BF16)
         return cols
 
@@ -324,30 +337,8 @@
         m_two[a] = total_two.astype(BF16)
         m_one[a] = total_one.astype(BF16)
 
-    settle(recv_sem, 0, xr, yr, xyr, zr)
-    cols = build_planes(0, lambda x: inner[x], xr, yr, xyr, zr)
-
-    back = nn(m_two[0], planes[:, 256:768]) + nn(m_two[1], planes[:, 128:640]) + nn(m_two[2], planes[:, 0:512])
-    delta = jnp.where(acts[...].astype(F32) > 0, back, back * 0.3).astype(BF16)
-    wide_delta = delta.astype(F32)
-    bias_one = wide_delta[:, 0:128] + wide_delta[:, 128:256] + wide_delta[:, 256:384] + wide_delta[:, 384:512]
-
-    def delta_at(x):
-        return delta[:, x * 128 : (x + 1) * 128]
-
-    xs2[0] = delta_at(0)
-    xs2[1] = delta_at(3)
-    for h in range(2):
-        for at, x in ((0, 0), (1, 3), (2, 1), (3, 2)):
-            ys2[h, at * 16 : at * 16 + 16] = delta_at(x)[112 * h : 112 * h + 16]
-    z_face = nt(ends, jnp.concatenate([delta_at(x) for x in range(4)], axis=0))
-    z_edge = nt(ends, edge_rows(delta_at))
-    for f in range(2):
-        face = [z_face[f : f + 1, x * 128 : (x + 1) * 128] for x in range(4)]
-        zs2[f] = stack8([face[1], face[2], face[0], face[3], z_edge[f : f + 1]])
-    exchange(1, xs2, xr2, ys2, yr2, xyr2, zs2, zr2)
-    for x in range(4):
-        inner[x] = delta_at(x)
+    settle(recv_sem, 0, (1, 2, 3), xr, yr, xyr, zr)
+    build_planes(0, lambda x: inner[x], xr, yr, xyr)
 
     v_tiles = jnp.concatenate(
         [yr[0, 16:32], yr[1, 16:32]]
@@ -355,34 +346,50 @@
         axis=0,
     )
     rims = nn(const("rim_rows")[:, 0:96], v_tiles)
+    volp[120:128, :] = jnp.zeros((8, 768), F32)
+    for p in range(6):
+        mid = vol_rows(p - 1) if 1 <= p <= 4 else xr[p // 5, 128:160].astype(F32)
+        plane = jnp.concatenate([mid, rims[p * 8 : p * 8 + 8]], axis=0)
+        lanes = slice(p * 128, (p + 1) * 128)
+        volp[40:80, lanes] = plane
+        volp[0:40, lanes] = pltpu.roll(plane, 1, 1)
+        volp[80:120, lanes] = pltpu.roll(plane, 127, 1)
+
+    settle(recv_sem, 0, (0,), xr, yr, xyr, zr)
+    cols = close_planes(0, zr)
+
+    back = nn(m_two[0], planes[:, 256:768]) + nn(m_two[1], planes[:, 128:640]) + nn(m_two[2], planes[:, 0:512])
+    delta = jnp.where(acts[...].astype(F32) > 0, back, back * 0.3).astype(BF16)
+    wide_delta = delta.astype(F32)
+    bias_one = wide_delta[:, 0:128] + wide_delta[:, 128:256] + wide_delta[:, 256:384] + wide_delta[:, 384:512]
+
+    def delta_at(x):
+        return delta[:, x * 128 : (x + 1) * 128]
+
     rim_cols = nn(const("rim_cols"), cols.astype(BF16))
     lane40 = lax.broadcasted_iota(jnp.int32, (40, 128), 1)
     half8 = lax.broadcasted_iota(jnp.int32, (8, 1), 0) < 4
-    volp[120:128, :] = jnp.zeros((8, 768), F32)
     for p in range(6):
         x = (p - 1) % 4
         dx = -1 if p == 0 else (1 if p == 5 else 0)
-        mid = vol_rows(x) if dx == 0 else xr[(dx + 1) // 2, 128:160].astype(F32)
-        plane = jnp.concatenate([mid, rims[p * 8 : p * 8 + 8]], axis=0)
         lanes = slice(p * 128, (p + 1) * 128)
-        volp[40:80, lanes] = plane
         r = {-1: 0, 1: 1, 0: 1}[dx]
-        for tap, side, turn, lane in ((0, 0, 1, 0), (2, 1, 127, 127)):
+        for tap, side, lane in ((0, 0, 0), (2, 1, 127)):
             k = 72 * side + 8 * way(dx, 0) + (3 if dx == 0 else r)
+            low, high = (72 * side + 8 * way(dx, e) + r for e in (-1, 1))
             col = jnp.concatenate(
                 [cols[j * 32 + x * 8 : j * 32 + x * 8 + 8, k : k + 1] for j in range(4)]
                 + [
                     jnp.where(
                         half8,
-                        rim_cols[p * 8 : p * 8 + 8, 72 * side + 8 * way(dx, -1) + r : 72 * side + 8 * way(dx, -1) + r + 1],
-                        rim_cols[p * 8 : p * 8 + 8, 72 * side + 8 * way(dx, 1) + r : 72 * side + 8 * way(dx, 1) + r + 1],
+                        rim_cols[p * 8 : p * 8 + 8, low : low + 1],
+                        rim_cols[p * 8 : p * 8 + 8, high : high + 1],
                     )
                 ],
                 axis=0,
             )
-            volp[tap * 40 : tap * 40 + 40, lanes] = jnp.where(
-                lane40 == lane, jnp.broadcast_to(col, (40, 128)), pltpu.roll(plane, turn, 1)
-            )
+            rows = slice(tap * 40, tap * 40 + 40)
+            volp[rows, lanes] = jnp.where(lane40 == lane, jnp.broadcast_to(col, (40, 128)), volp[rows, lanes])
 
     y_of = const("y_of").astype(F32)
     sums = []
@@ -437,6 +444,20 @@
     own.start()
     own.wait()
 
+    xs2[0] = delta_at(0)
+    xs2[1] = delta_at(3)
+    for h in range(2):
+        for at, x in ((0, 0), (1, 3), (2, 1), (3, 2)):
+            ys2[h, at * 16 : at * 16 + 16] = delta_at(x)[112 * h : 112 * h + 16]
+    z_face = nt(ends, jnp.concatenate([delta_at(x) for x in range(4)], axis=0))
+    z_edge = nt(ends, edge_rows(delta_at))
+    for f in range(2):
+        face = [z_face[f : f + 1, x * 128 : (x + 1) * 128] for x in range(4)]
+        zs2[f] = stack8([face[1], face[2], face[0], face[3], z_edge[f : f + 1]])
+    exchange(1, xs2, xr2, ys2, yr2, xyr2, zs2, zr2)
+    for x in range(4):
+        inner[x] = delta_at(x)
+
     def await_rows(sem, ref, n):
         ref = ref.at[pl.ds(0, n * ROWS)]
         pltpu.make_async_copy(ref, ref, sem).wait()
@@ -459,13 +480,6 @@
     own.start()
     own.wait()
 
-    settle(recv_sem, 1, xr2, yr2, xyr2, zr2)
-    build_planes(1, lambda x: inner[x], xr2, yr2, xyr2, zr2)
-    grad = nn(m_one[0], planes[:, 256:768]) + nn(m_one[1], planes[:, 128:640]) + nn(m_one[2], planes[:, 0:512])
-    for j in range(4):
-        for x in range(4):
-            gvol[j, x] = grad[j * 8 : j * 8 + 8, x * 128 : (x + 1) * 128]
-
     await_rows(red_recv.at[1], got2, n_line - 1)
     mid2[...] = total8(got2, n_line) * norm
 
@@ -477,8 +491,16 @@
     own = pltpu.make_async_copy(mid2.at[pl.ds(0, ROWS)], summed.at[pl.ds(ROWS * group_at, ROWS)], own_sem.at[2])
     own.start()
     own.wait()
-    settle(send_sem, 0, xr, yr, xyr, zr)
-    settle(send_sem, 1, xr2, yr2, xyr2, zr2)
+    settle(recv_sem, 1, range(4), xr2, yr2, xyr2, zr2)
+    build_planes(1, lambda x: inner[x], xr2, yr2, xyr2)
+    close_planes(1, zr2)
+    grad = nn(m_one[0], planes[:, 256:768]) + nn(m_one[1], planes[:, 128:640]) + nn(m_one[2], planes[:, 0:512])
+    for j in range(4):
+        for x in range(4):
+            gvol[j, x] = grad[j * 8 : j * 8 + 8, x * 128 : (x + 1) * 128]
+
+    settle(send_sem, 0, range(4), xr, yr, xyr, zr)
+    settle(send_sem, 1, range(4), xr2, yr2, xyr2, zr2)
     await_rows(red_send.at[0], got1, n_group - 1)
     await_rows(red_send.at[1], got2, n_line - 1)
     await_rows(red_recv.at[2], summed, n_group - 1)
@@ -536,7 +558,7 @@
             buf(NARROW, 128), buf(208, 512), buf(1152, 128),
             buf(2, 160, 128), buf(2, 160, 128), buf(2, 80, 128), buf(2, 80, 128), buf(4, 32, 128), buf32(2, 8, 128), buf32(2, 72, 128),
             buf(2, 128, 128), buf(2, 128, 128), buf(2, 64, 128), buf(2, 64, 128), buf(4, 16, 128), buf32(2, 8, 128), buf32(2, 72, 128),
-            buf(4, 128, 128), buf(128, 512), buf(512, 768), buf32(128, 768), buf(3, 128, 512), buf(3, 32, 512),
+            buf(4, 128, 128), buf(128, 512), buf(512, 768), buf32(2, 160, 768), buf32(128, 768), buf(3, 128, 512), buf(3, 32, 512),
             buf32(96, 128), buf32(4 * n_group, 128), buf32(4 * n_line, 128), buf32(8, 128), buf32(8, 128),
             pltpu.SemaphoreType.DMA((9,)), pltpu.SemaphoreType.DMA((3,)),
             pltpu.SemaphoreType.DMA((2, 4)), pltpu.SemaphoreType.DMA((2, 4)),

time: 48.4 us -> 47.9 us (0.990)
  Pallas kernels: 47.6 us -> 47.1 us
where the time goes in v4:
time: 47.9 us; the launch traced here: 47.8 us
  Pallas kernels  47.1 us (98%)
  between operations  0.64 us (1%)
    pallas_call x1, Pallas kernels, local(): pl.pallas_call(functools.partial(kernel, sizes, norm), out_shape=(pltpu.V...  46.3 us

profile of v4, /device:TPU:1, one launch (start us, length us, event | category | flops | bytes accessed | tf_op | source)
XLA Modules:
  0.0 47.8 jit_solution(200504689544876106)
XLA Ops:
  0.6 46.3 %both_layers.1 = (f32[96,128]{1,0:T(8,128)S(1)}, f32[4,4,8,128]{3,2,1,0:T(8,128)S(1)}) custom-call(bf16[4,4,8,128]{3,2,1,0:T(8,128)(2,1)} %vol_h.1, bf16[16,4,8,128]{3,2,1,0:T(8,128)(2,1)} %act1_h.1, bf16[16,4,8,128]{3,2,1,0:T(8,128)(2,1)} %act2_h.1, bf16[27,4,16]{2,1,0:T(4,128)(2,1)} %bitcast.13, bf16[27,16,16]{2,1,0:T(8,128)(2,1)} %bitcast.12, ...), custom_call_target="tpu_custom_call" | custom-call | tf_op jit(solution)/shard_map/both_layers/pallas_call | solution.py:548
  46.9 0.9 %finish.1 = (f32[27,4,16]{2,1,0:T(4,128)}, f32[16]{0:T(128)}, f32[27,16,16]{2,1,0:T(8,128)}, f32[16]{0:T(128)}, f32[4,4,8,128]{3,2,1,0:T(8,128)}) custom-call(f32[96,128]{1,0:T(8,128)S(1)} %get-tuple-element.12.summed, f32[4,4,8,128]{3,2,1,0:T(8,128)S(1)} %get-tuple-element.13.gvol_v), custom_call_target="tpu_custom_call" | custom-call | tf_op jit(solution)/shard_map/finish/pallas_call | solution.py:571
